TPU v7x, 256 devices: a whole 4x4x8 slice. The times are simulated.
256 devices in a mesh: island: 8 (over z_hi, x), row: 8 (over y, core), col: 4 (over z_lo).
Axes of the slice: x: 4, y: 4, z: 8 (z_hi: 2, z_lo: 4; z = z_hi * 4 + z_lo), core: 2. Of those that a mesh axis runs over, the one named last changes fastest.
Arguments:
- deltas: float32 [8, 4096, 8192], P('island', 'row', 'col'), may hold values from -0.26516503 to 0.26516503
- left_stat: float32 [4096, 4096], P(('island', 'col'), 'row'), may hold values from -1.5 to 1.5
- right_stat: float32 [8192, 8192], P(('island', 'row'), 'col'), may hold values from -1.5 to 1.5
Outputs:
- left_new: float32 [4096, 4096], P(('island', 'col'), 'row')
- right_new: float32 [8192, 8192], P(('island', 'row'), 'col')
All inputs are finite; a program needn't handle non-finite values.
Results may differ from a plain program's by a relative error of at most 0.00037.
Values may be sent and summed in bfloat16 or wider, within the bound.
No kernel may reach another device: no remote copies, remote signals or barrier semaphores. Data moves between devices by JAX's collectives and lax.ppermute only.
A program may use at most 64 MiB of HBM per device.

v0:
```python
import jax
import jax.numpy as jnp
from jax import lax
from jax.sharding import PartitionSpec as P

M = 4096
N = 8192


def padded_to(lines, count):
    spare = -lines.shape[0] % count
    if not spare:
        return lines
    return jnp.concatenate([lines, jnp.zeros((spare, *lines.shape[1:]), lines.dtype)])


def broadcast_by_parts(shard, axis, root):
    lines = jnp.where(lax.axis_index(axis) == root, shard, jnp.zeros_like(shard)).reshape(
        -1, *shard.shape[1:][-1:]
    )
    padded = padded_to(lines, lax.axis_size(axis))
    own = lax.psum_scatter(padded, axis, scatter_dimension=0, tiled=True)
    return lax.all_gather(own, axis, axis=0, tiled=True)[: len(lines)].reshape(shard.shape)


def split_up(shard, dim, count):
    before, after = (shard.shape[:dim], shard.shape[dim + 1 :])
    return jnp.moveaxis(shard.reshape(*before, count, -1, *after), dim, 0)


def summed_on_arrival(shard, axis, dim):
    tiles = split_up(shard, dim, lax.axis_size(axis))
    arrived = lax.all_to_all(tiles, axis, split_axis=0, concat_axis=0, tiled=True)
    return arrived.sum(axis=0)


def from_root(shard, axis, root):
    return lax.dynamic_index_in_dim(lax.all_gather(shard, axis), root, 0, keepdims=False)


def local(deltas, left_stat, right_stat):
    islands = lax.axis_size("island")
    island = lax.axis_index("island")
    local_delta = deltas[0]
    shares = lax.psum_scatter(local_delta, "island", scatter_dimension=0, tiled=True)
    rounded = (shares / islands).astype(jnp.bfloat16)
    panel = lax.all_gather(rounded, "island", axis=0, tiled=True)
    rows_local = panel.shape[0]
    rows_island = M // islands
    row_extent = min(rows_island, rows_local)
    number = 0
    start_row = island * rows_island + number * row_extent
    source = start_row // rows_local
    segment = panel
    blocks = broadcast_by_parts(segment, "row", source)
    left_tile = lax.dot_general(
        blocks, panel, (((1,), (1,)), ((), ())), preferred_element_type=jnp.float32
    )
    left_shares = summed_on_arrival(left_tile, "col", 0)
    left_new = left_stat + left_shares
    cols_local = panel.shape[1]
    cols_island = N // islands
    col_extent = min(cols_island, cols_local)
    number = 0
    start_col = island * cols_island + number * col_extent
    source = start_col // cols_local
    offset = start_col - source * cols_local
    segment = lax.dynamic_slice_in_dim(panel, offset, col_extent, 1)
    columns = from_root(segment, "col", source)
    right_tile = lax.dot_general(
        columns, panel, (((0,), (0,)), ((), ())), preferred_element_type=jnp.float32
    )
    right_shares = lax.psum_scatter(right_tile, "row", scatter_dimension=0, tiled=True)
    right_new = right_stat + right_shares
    return (left_new, right_new)


def solution(mesh):
    in_specs = (P("island", "row", "col"), P(("island", "col"), "row"), P(("island", "row"), "col"))
    out_specs = (P(("island", "col"), "row"), P(("island", "row"), "col"))
    return jax.shard_map(local, mesh=mesh, in_specs=in_specs, out_specs=out_specs, check_vma=False)
```

profile of v0, /device:TPU:1, one launch (start us, length us, event | category | flops | bytes accessed | tf_op | source)
XLA Modules:
  0.0 430.5 jit_solution(14289214902869584653)
XLA Ops:
  7.2 0.0 reduce-scatter.4.cloned.1.call-start
  7.2 0.7 reduce-scatter.4.cloned.1.call-update
  7.9 0.0 all-gather.5.cloned.1.call-start
  7.9 129.9 %reduce-scatter.4.cloned.1.call-done = f32[64,2048]{1,0:T(8,128)} async-done(((f32[512,2048]{1,0:T(8,128)}), f32[64,2048]{1,0:T(8,128)}) %reduce-scatter.4.cloned.1.call-update) | async-done | bytes 524304 | tf_op jit(solution)/shard_map/reduce_scatter | solution.py:45
  137.9 1.8 multiply_convert_fusion
  139.6 0.0 all-gather.5.cloned.1.call-update
  139.7 0.0 reduce-scatter.6.cloned.1.call-start
  139.7 72.0 %all-gather.5.cloned.1.call-done = bf16[512,2048]{1,0:T(8,128)(2,1)} async-done(((bf16[64,2048]{1,0:T(8,128)(2,1)}), bf16[512,2048]{1,0:T(8,128)(2,1)}) %all-gather.5.cloned.1.call-update) | async-done | bytes 2097168 | tf_op jit(solution)/shard_map/all_gather | solution.py:47
  211.7 1.5 broadcast_select_fusion
  213.2 0.0 reduce-scatter.6.cloned.1.call-update
  213.2 0.0 all-gather.9.cloned.1.call-start
  213.3 1.5 copy-done
  214.8 1.1 constant_dynamic-slice_fusion
  215.9 0.0 all-gather.9.cloned.1.call-update
  215.9 0.0 all-gather.7.cloned.1.call-start
  215.9 30.9 %reduce-scatter.6.cloned.1.call-done = bf16[64,2048]{1,0:T(8,128)(2,1)} async-done(((bf16[512,2048]{1,0:T(8,128)(2,1)}), bf16[64,2048]{1,0:T(8,128)(2,1)}) %reduce-scatter.6.cloned.1.call-update) | async-done | bytes 262160 | tf_op jit(solution)/shard_map/reduce_scatter | solution.py:22
  246.8 0.0 all-gather.7.cloned.1.call-update
  246.8 0.0 reduce-scatter.8.cloned.1.call-start
  246.9 87.2 %all-gather.9.cloned.1.call-done = bf16[2048,1024]{1,0:T(8,128)(2,1)} async-done(((bf16[512,1024]{1,0:T(8,128)(2,1)}), bf16[2048,1024]{1,0:T(8,128)(2,1)}) %all-gather.9.cloned.1.call-update) | async-done | bytes 4194320 | tf_op jit(solution)/shard_map/all_gather | solution.py:38
  334.1 6.8 %fusion = f32[1024,2048]{1,0:T(8,128)} fusion(bf16[512,2048]{1,0:T(8,128)(2,1)S(1)} %copy-done, bf16[4,512,1024]{2,1,0:T(8,128)(2,1)} %bitcast.11, s32[]{:T(128)S(6)} %select_n.28), kind=kOutput, calls=%fused_computation.1 | convolution fusion | flops 2147483648 | bytes 11534340 | tf_op jit(solution)/shard_map/dot_general | solution.py:70
  340.9 0.0 reduce-scatter.8.cloned.1.call-update
  340.9 23.5 %all-gather.7.cloned.1.call-done = bf16[512,2048]{1,0:T(8,128)(2,1)} async-done(((bf16[64,2048]{1,0:T(8,128)(2,1)}), bf16[512,2048]{1,0:T(8,128)(2,1)}) %all-gather.7.cloned.1.call-update) | async-done | bytes 2097168 | tf_op jit(solution)/shard_map/all_gather | solution.py:23
  364.4 2.9 fusion.4
  367.3 0.0 copy-start.2
  367.3 0.0 copy-start.1
  367.3 29.8 %all_to_all.5 = f32[4,128,512]{2,1,0:T(8,128)S(1)} all-to-all(f32[4,128,512]{2,1,0:T(8,128)S(1)} %bitcast.10), channel_id=1, replica_groups=mesh['island'=8,'row'=8,'col'=4] {'col'}, dimensions={0} | all-to-all | bytes 2097152 | tf_op jit(solution)/shard_map/all_to_all | solution.py:33
  397.2 0.1 reduce_sum.9
  397.3 0.0 copy-done.2
  397.3 0.7 add.21
  398.0 23.3 %reduce-scatter.8.cloned.1.call-done = f32[128,2048]{1,0:T(8,128)} async-done(((f32[1024,2048]{1,0:T(8,128)}), f32[128,2048]{1,0:T(8,128)}) %reduce-scatter.8.cloned.1.call-update) | async-done | bytes 1048592 | tf_op jit(solution)/shard_map/reduce_scatter | solution.py:73
  421.3 0.0 copy-done.1
  421.3 2.3 add.24
  (1 shorter events, 0.0 us)
Async XLA Ops:
  7.2 130.7 %reduce-scatter.4.cloned.1.call-start = ((), (), s32[]{:S(2)}) async-start(), calls=%async_computation.4 | async-start | bytes 4718592 | tf_op jit(solution)/shard_map/reduce_scatter | solution.py:45
  7.9 203.8 %all-gather.5.cloned.1.call-start = ((), (), s32[]{:S(2)}) async-start(), calls=%async_computation.5 | async-start | bytes 2359296 | tf_op jit(solution)/shard_map/all_gather | solution.py:47
  139.7 107.1 %reduce-scatter.6.cloned.1.call-start = ((), (), s32[]{:S(2)}) async-start(), calls=%async_computation.6 | async-start | bytes 2359296 | tf_op jit(solution)/shard_map/reduce_scatter | solution.py:22
  213.2 1.6 copy-start
  213.2 120.9 %all-gather.9.cloned.1.call-start = ((), (), s32[]{:S(2)}) async-start(), calls=%async_computation.9 | async-start | bytes 5242880 | tf_op jit(solution)/shard_map/all_gather | solution.py:38
  215.9 148.5 %all-gather.7.cloned.1.call-start = ((), (), s32[]{:S(2)}) async-start(), calls=%async_computation.7 | async-start | bytes 2359296 | tf_op jit(solution)/shard_map/all_gather | solution.py:23
  246.8 174.5 %reduce-scatter.8.cloned.1.call-start = ((), (), s32[]{:S(2)}) async-start(), calls=%async_computation.8 | async-start | bytes 9437184 | tf_op jit(solution)/shard_map/reduce_scatter | solution.py:73
  367.3 30.0 %copy-start.2 = (f32[128,512]{1,0:T(8,128)S(1)}, f32[128,512]{1,0:T(8,128)}, u32[]{:S(2)}) copy-start(f32[128,512]{1,0:T(8,128)} %param.4) | copy-start | bytes 786436
  367.3 54.0 %copy-start.1 = (f32[128,2048]{1,0:T(8,128)S(1)}, f32[128,2048]{1,0:T(8,128)}, u32[]{:S(2)}) copy-start(f32[128,2048]{1,0:T(8,128)} %param.5) | copy-start | bytes 3145732
Sparse Core Ops, SparseCore 0:
  12.1 125.6 reduce-scatter.3
  141.1 70.6 all-gather.4
  214.3 32.4 reduce-scatter.5
  249.0 84.9 all-gather.8
  335.8 28.5 all-gather.6
  366.8 54.4 reduce-scatter.7
where the time goes:
time: 431 us; the launch traced here: 430 us
  waiting for transfers between devices  368 us (85%)
  blocking collectives  29.8 us (7%)
  between operations  14.2 us (3%)
  matrix products  9.71 us (2%)
  other arithmetic  6.39 us (1%)
    reduce_scatter x1, waiting for transfers between devices, local(): lax.psum_scatter(local_delta, 'island', scatter_dimension=0, tiled=True)  130 us
    all_gather x1, waiting for transfers between devices, from_root(): lax.all_gather(shard, axis)  87.2 us
    all_gather x1, waiting for transfers between devices, local(): panel = lax.all_gather(rounded, 'island', axis=0, tiled=True)  72 us
    reduce_scatter x1, waiting for transfers between devices, broadcast_by_parts(): own = lax.psum_scatter(padded, axis, scatter_dimension=0, tiled=True)  30.9 us
    all_to_all x1, blocking collectives, summed_on_arrival(): lax.all_to_all(tiles, axis, split_axis=0, concat_axis=0, tiled=True)  29.8 us
    all_gather x1, waiting for transfers between devices, broadcast_by_parts(): lax.all_gather(own, axis, axis=0, tiled=True)[:len(lines)]  23.5 us
    reduce_scatter x1, waiting for transfers between devices, local(): lax.psum_scatter(right_tile, 'row', scatter_dimension=0, tiled=True)  23.3 us
  transfers between devices with their start and end apart: 6, of which 6 were waited for; matrix products, arithmetic and copies ran while one was open for 3% of the time, Pallas kernels for 0%

commit v1 on v0

--- a/solution.py
+++ b/solution.py
@@ -20,7 +20,9 @@
     )
     padded = padded_to(lines, lax.axis_size(axis))
     own = lax.psum_scatter(padded, axis, scatter_dimension=0, tiled=True)
-    return lax.all_gather(own, axis, axis=0, tiled=True)[: len(lines)].reshape(shard.shape)
+    return jnp.concatenate(
+        lax.all_to_all(jnp.stack([own] * lax.axis_size(axis)), axis, 0, 0), axis=0
+    )[: len(lines)].reshape(shard.shape)
 
 
 def split_up(shard, dim, count):

time: 431 us -> 415 us (0.963)
  waiting for transfers between devices: 368 us -> 314 us
  blocking collectives: 29.8 us -> 68.9 us
    all_to_all x0 -> x1, blocking collectives: none -> 39.2 us  [broadcast_by_parts(): lax.all_to_all(jnp.stack([own] * lax.axis_size(axis)), axis, 0, 0)]
    all_gather x1 -> x0, waiting for transfers between devices: 23.5 us -> none  [broadcast_by_parts(): lax.all_gather(own, axis, axis=0, tiled=True)[:len(lines)]]
    reduce_scatter x1, waiting for transfers between devices: 23.3 us -> 0.56 us  [local(): lax.psum_scatter(right_tile, 'row', scatter_dimension=0, tiled=True)]
    all_gather x1, waiting for transfers between devices: 87.2 us -> 80.8 us  [from_root(): lax.all_gather(shard, axis)]
  transfers between devices with their start and end apart: 6 -> 5, of which waited for: 6 -> 5; matrix products, arithmetic and copies ran while one was open for 3% -> 3% of each run, Pallas kernels for 0% -> 0%
where the time goes in v1:
time: 415 us
  waiting for transfers between devices  314 us (76%)
  blocking collectives  68.9 us (17%)
  between operations  13.9 us (3%)
  matrix products  8.12 us (2%)
  other arithmetic  6.38 us (2%)
    reduce_scatter x1, waiting for transfers between devices, local(): lax.psum_scatter(local_delta, 'island', scatter_dimension=0, tiled=True)  130 us
    all_gather x1, waiting for transfers between devices, from_root(): lax.all_gather(shard, axis)  80.8 us
    all_gather x1, waiting for transfers between devices, local(): panel = lax.all_gather(rounded, 'island', axis=0, tiled=True)  72 us
    all_to_all x1, blocking collectives, broadcast_by_parts(): lax.all_to_all(jnp.stack([own] * lax.axis_size(axis)), axis, 0, 0)  39.2 us
    reduce_scatter x1, waiting for transfers between devices, broadcast_by_parts(): own = lax.psum_scatter(padded, axis, scatter_dimension=0, tiled=True)  29.9 us
    all_to_all x1, blocking collectives, summed_on_arrival(): lax.all_to_all(tiles, axis, split_axis=0, concat_axis=0, tiled=True)  29.7 us
  transfers between devices with their start and end apart: 5, of which 5 were waited for; matrix products, arithmetic and copies ran while one was open for 3% of the time, Pallas kernels for 0%

profile of v1, /device:TPU:1, one launch (start us, length us, event | category | flops | bytes accessed | tf_op | source)
XLA Modules:
  0.0 414.9 jit_solution(16547493332652149022)
XLA Ops:
  7.2 0.0 reduce-scatter.4.cloned.1.call-start
  7.2 0.7 reduce-scatter.4.cloned.1.call-update
  7.9 0.0 all-gather.4.cloned.1.call-start
  7.9 129.9 %reduce-scatter.4.cloned.1.call-done = f32[64,2048]{1,0:T(8,128)} async-done(((f32[512,2048]{1,0:T(8,128)}), f32[64,2048]{1,0:T(8,128)}) %reduce-scatter.4.cloned.1.call-update) | async-done | bytes 524304 | tf_op jit(solution)/shard_map/reduce_scatter | solution.py:47
  137.9 1.8 multiply_convert_fusion
  139.6 0.0 all-gather.4.cloned.1.call-update
  139.7 0.0 all-gather.6.cloned.1.call-start
  139.7 72.0 %all-gather.4.cloned.1.call-done = bf16[512,2048]{1,0:T(8,128)(2,1)} async-done(((bf16[64,2048]{1,0:T(8,128)(2,1)}), bf16[512,2048]{1,0:T(8,128)(2,1)}) %all-gather.4.cloned.1.call-update) | async-done | bytes 2097168 | tf_op jit(solution)/shard_map/all_gather | solution.py:49
  211.7 0.0 copy-start
  211.7 2.4 constant_dynamic-slice_fusion
  214.1 0.0 all-gather.6.cloned.1.call-update
  214.2 0.0 reduce-scatter.6.cloned.1.call-start
  214.2 0.0 copy-done
  214.2 1.5 broadcast_select_fusion
  215.7 0.0 reduce-scatter.6.cloned.1.call-update
  215.7 0.0 reduce-scatter.8.cloned.1.call-start
  215.8 80.8 %all-gather.6.cloned.1.call-done = bf16[2048,1024]{1,0:T(8,128)(2,1)} async-done(((bf16[512,1024]{1,0:T(8,128)(2,1)}), bf16[2048,1024]{1,0:T(8,128)(2,1)}) %all-gather.6.cloned.1.call-update) | async-done | bytes 4194320 | tf_op jit(solution)/shard_map/all_gather | solution.py:40
  296.6 6.8 %fusion.2 = f32[1024,2048]{1,0:T(8,128)} fusion(bf16[512,2048]{1,0:T(8,128)(2,1)S(1)} %copy-done, bf16[4,512,1024]{2,1,0:T(8,128)(2,1)} %bitcast.13, s32[]{:T(128)S(6)} %select_n.28), kind=kOutput, calls=%fused_computation.3 | convolution fusion | flops 2147483648 | bytes 11534340 | tf_op jit(solution)/shard_map/dot_general | solution.py:72
  303.4 0.0 reduce-scatter.8.cloned.1.call-update
  303.4 29.9 %reduce-scatter.6.cloned.1.call-done = bf16[64,2048]{1,0:T(8,128)(2,1)} async-done(((bf16[512,2048]{1,0:T(8,128)(2,1)}), bf16[64,2048]{1,0:T(8,128)(2,1)}) %reduce-scatter.6.cloned.1.call-update) | async-done | bytes 262160 | tf_op jit(solution)/shard_map/reduce_scatter | solution.py:22
  333.3 1.2 stack.2
  334.5 39.2 %all_to_all.10 = bf16[8,64,2048]{2,1,0:T(8,128)(2,1)S(1)} all-to-all(bf16[8,64,2048]{2,1,0:T(8,128)(2,1)S(1)} %stack.2), channel_id=1, replica_groups=mesh['island'=8,'row'=8,'col'=4] {'row'}, dimensions={0} | all-to-all | bytes 4194304 | tf_op jit(solution)/shard_map/all_to_all | solution.py:24
  373.7 1.3 fusion
  375.0 0.0 copy-start.2
  375.0 0.0 copy-start.1
  375.0 29.7 %all_to_all.11 = f32[4,128,512]{2,1,0:T(8,128)S(1)} all-to-all(f32[4,128,512]{2,1,0:T(8,128)S(1)} %fusion), channel_id=1, replica_groups=mesh['island'=8,'row'=8,'col'=4] {'col'}, dimensions={0} | all-to-all | bytes 2097152 | tf_op jit(solution)/shard_map/all_to_all | solution.py:35
  404.7 0.1 reduce_sum.9
  404.8 0.0 copy-done.2
  404.8 0.7 add.21
  405.5 0.6 reduce-scatter.8.cloned.1.call-done
  406.1 0.0 copy-done.1
  406.1 2.3 add.24
Async XLA Ops:
  7.2 130.7 %reduce-scatter.4.cloned.1.call-start = ((), (), s32[]{:S(2)}) async-start(), calls=%async_computation.5 | async-start | bytes 4718592 | tf_op jit(solution)/shard_map/reduce_scatter | solution.py:47
  7.9 203.8 %all-gather.4.cloned.1.call-start = ((), (), s32[]{:S(2)}) async-start(), calls=%async_computation.6 | async-start | bytes 2359296 | tf_op jit(solution)/shard_map/all_gather | solution.py:49
  139.7 156.9 %all-gather.6.cloned.1.call-start = ((), (), s32[]{:S(2)}) async-start(), calls=%async_computation.9 | async-start | bytes 5242880 | tf_op jit(solution)/shard_map/all_gather | solution.py:40
  211.7 2.5 copy-start
  214.2 119.1 %reduce-scatter.6.cloned.1.call-start = ((), (), s32[]{:S(2)}) async-start(), calls=%async_computation.7 | async-start | bytes 2359296 | tf_op jit(solution)/shard_map/reduce_scatter | solution.py:22
  215.7 190.4 %reduce-scatter.8.cloned.1.call-start = ((), (), s32[]{:S(2)}) async-start(), calls=%async_computation.8 | async-start | bytes 9437184 | tf_op jit(solution)/shard_map/reduce_scatter | solution.py:75
  375.0 29.8 %copy-start.2 = (f32[128,512]{1,0:T(8,128)S(1)}, f32[128,512]{1,0:T(8,128)}, u32[]{:S(2)}) copy-start(f32[128,512]{1,0:T(8,128)} %param.4) | copy-start | bytes 786436
  375.0 31.1 %copy-start.1 = (f32[128,2048]{1,0:T(8,128)S(1)}, f32[128,2048]{1,0:T(8,128)}, u32[]{:S(2)}) copy-start(f32[128,2048]{1,0:T(8,128)} %param.5) | copy-start | bytes 3145732
Sparse Core Ops, SparseCore 0:
  12.1 125.6 reduce-scatter.3
  141.1 70.6 all-gather.3
  214.3 82.2 all-gather.5
  299.0 34.2 reduce-scatter.5
  335.7 70.3 reduce-scatter.7
